TPU v7x, 128 devices: a whole 4x4x4 slice. The times are simulated.
128 devices in a mesh: sp: 8 (over x, y_lo), ep: 16 (over z, y_hi, core).
Axes of the slice: x: 4, y: 4 (y_hi: 2, y_lo: 2; y = y_hi * 2 + y_lo), z: 4, core: 2. Of those that a mesh axis runs over, the one named last changes fastest.
Arguments:
- residual: bfloat16 [16384, 4096], P(('sp', 'ep')), may hold values from -40 to 40
- queries: bfloat16 [16384, 4096], P(('sp', 'ep')), may hold values from -6 to 6
- key_rows: bfloat16 [16384, 1024], P(('sp', 'ep')), may hold values from -6 to 6
- value_rows: bfloat16 [16384, 1024], P(('sp', 'ep')), may hold values from -6 to 6
- visible: int32 [128, 9], replicated, may hold values from 0 to 1, as said below
- out_proj: bfloat16 [4096, 4096], P(('sp', 'ep')), may hold values from -0.09375 to 0.09375
- norm_gain: float32 [4096], replicated, may hold values from 0.5 to 1.5
- expert_ids: int32 [16384, 2], P(('sp', 'ep')), may hold values from 0 to 7, all different within a row; in each aligned block of 128 rows (0 to 127, 128 to 255, ...) at most 40 rows name the same one
- route_weight: float32 [16384, 2], P(('sp', 'ep')), may hold values from 0.2 to 1
- expert_gate: bfloat16 [2, 7168, 4096], P(None, 'ep'), may hold values from -0.09375 to 0.09375
- expert_up: bfloat16 [2, 7168, 4096], P(None, 'ep'), may hold values from -0.09375 to 0.09375
- expert_down: bfloat16 [2, 7168, 4096], P(None, 'ep'), may hold values from -0.0625 to 0.0625
Outputs:
- layer_out: bfloat16 [16384, 4096], P(('sp', 'ep'))
Inputs may be any that keep to these rules, and one draw needn't show every extreme that they name: The sequence is packed with documents that are runs of whole blocks of 128 tokens, the first of them 9 blocks or longer; visible[q, d] is 1 exactly when block q - d exists and lies in the document of block q, so visible[q, 0] = 1. `expert_ids`: each token names two different experts. Among the 128 tokens of one block no expert is named by more than 40 tokens.
All inputs are finite; a program needn't handle non-finite values.
Results may differ from a plain program's by a relative error of at most 0.0065.
Values may be sent and summed in bfloat16 or wider, within the bound.
No kernel may reach another device: no remote copies, remote signals or barrier semaphores. Data moves between devices by JAX's collectives and lax.ppermute only.
A program may use at most 128 MiB of HBM per device.

v0:
```python
import math
import jax
import jax.numpy as jnp
from jax import lax
from jax.sharding import Mesh
from jax.sharding import PartitionSpec as P

HEAD = 128
CAP = 40
SP = ("sp_0", "sp_1")
EP = ("ep_0", "ep_1", "ep_2")
SP_EP = ("sp_0", "sp_1", "ep_0", "ep_1", "ep_2")


def shifted(value, axis, steps):
    count = lax.axis_size(axis)
    pairs = [(source, (source + steps) % count) for source in range(count)]
    return lax.ppermute(value, axis, pairs)


def sum_by_axis(terms, axes):
    total = terms.astype(jnp.bfloat16)
    for axis in axes:
        total = lax.psum_scatter(total, axis, scatter_dimension=0, tiled=True)
    return total.astype(jnp.float32)


def split_up(array, dim, size):
    before, after = (array.shape[:dim], array.shape[dim + 1 :])
    return jnp.moveaxis(array.reshape(*before, size, -1, *after), dim, 0)


def summed_rows(array, chips, core, dim):
    sizes = (lax.axis_size(chips), lax.axis_size(core))
    blocks = split_up(array, dim, sizes[0] * sizes[1])
    inside = blocks.shape[1:]
    blocks = blocks.reshape(*sizes, *inside).swapaxes(0, 1).reshape(-1, *inside)
    blocks = lax.psum_scatter(blocks, core, scatter_dimension=0, tiled=True)
    return lax.psum_scatter(blocks, chips, scatter_dimension=0, tiled=True)[0]


def settle(shard_piece, distance, ep_index):
    lowered = jnp.concatenate([jnp.zeros_like(shard_piece[:1]), shard_piece[:-1]], axis=0)
    return jnp.where(distance > ep_index, lowered, shard_piece)


def local(
    residual,
    queries,
    key_rows,
    value_rows,
    visible,
    out_proj,
    norm_gain,
    expert_ids,
    route_weight,
    expert_gate,
    expert_up,
    expert_down,
):
    sp_count = lax.axis_size(SP)
    ep_count = lax.axis_size(EP)
    ep_index = lax.axis_index(EP)
    tokens = residual.shape[0]
    reach = ep_count // 2 + 1
    query_width = queries.shape[1] // sp_count
    key_width = key_rows.shape[1] // sp_count
    key_heads = key_width // HEAD
    grouping = query_width // key_width
    query_send = queries.reshape(1, tokens, sp_count, query_width)
    key_send = key_rows.reshape(1, tokens, sp_count, key_width)
    value_send = value_rows.reshape(1, tokens, sp_count, key_width)
    query_heads, key_local, value_local = (
        lax.all_to_all(query_send, SP, split_axis=2, concat_axis=0, tiled=True),
        lax.all_to_all(key_send, SP, split_axis=2, concat_axis=0, tiled=True),
        lax.all_to_all(value_send, SP, split_axis=2, concat_axis=0, tiled=True),
    )
    key_value = jnp.concatenate(
        [
            key_local.reshape(sp_count, tokens, key_width),
            value_local.reshape(sp_count, tokens, key_width),
        ],
        axis=2,
    )
    pieces = [key_value]
    for distance in range(1, reach):
        pieces.append(settle(shifted(key_value, EP, distance), distance, ep_index))
    window = jnp.stack(pieces, axis=0)
    key_window = window[..., :key_width].reshape(reach, sp_count, tokens, key_heads, HEAD)
    value_window = window[..., key_width:].reshape(reach, sp_count, tokens, key_heads, HEAD)
    query_local = query_heads.reshape(sp_count, tokens, key_heads, grouping, HEAD)
    scores = jnp.einsum(
        "stgrh,dsugh->sgrtdu", query_local, key_window, preferred_element_type=jnp.float32
    ) * (1.0 / math.sqrt(HEAD))
    seen = lax.dynamic_index_in_dim(
        visible.reshape(sp_count, ep_count, reach), ep_index, 1, keepdims=False
    )
    position = jnp.arange(tokens)
    distances = jnp.arange(reach)
    allowed = (seen[:, None, :, None] > 0) & (
        (distances[None, None, :, None] > 0)
        | (position[None, None, None, :] <= position[None, :, None, None])
    )
    allowed = allowed[:, None, None]
    scores = jnp.where(allowed, scores, -1e30)
    peak = jnp.max(scores, axis=(4, 5), keepdims=True)
    weights_f = jnp.where(allowed, jnp.exp(scores - peak), 0.0)
    totals = jnp.sum(weights_f, axis=(4, 5))
    weights_b = weights_f.astype(jnp.bfloat16)
    summed = jnp.einsum(
        "sgrtdu,dsugh->stgrh", weights_b, value_window, preferred_element_type=jnp.float32
    )
    attended = (summed / jnp.transpose(totals, (0, 3, 1, 2))[..., None]).astype(jnp.bfloat16)
    attended = attended.reshape(sp_count * tokens, query_width)
    proj_full = lax.all_gather(out_proj, EP, axis=0, tiled=True)
    projected = sum_by_axis(jnp.dot(attended, proj_full, preferred_element_type=jnp.float32), SP)
    hidden_sum = residual.astype(jnp.float32) + projected
    mean_square = jnp.mean(hidden_sum * hidden_sum, axis=-1, keepdims=True)
    normed = (hidden_sum * lax.rsqrt(mean_square + 1e-05) * norm_gain).astype(jnp.bfloat16)
    window_experts = expert_gate.shape[0]
    capacity = CAP
    choose = expert_ids[None] == jnp.arange(window_experts, dtype=jnp.int32)[:, None, None]
    member = jnp.any(choose, axis=2)
    token_weight = jnp.sum(jnp.where(choose, route_weight[None], 0.0), axis=2)
    ranked = jnp.cumsum(member.astype(jnp.int32), axis=1) - member.astype(jnp.int32)
    slot_hit = (
        ranked[:, None, :] == jnp.arange(capacity, dtype=jnp.int32)[None, :, None]
    ) & member[:, None, :]
    dispatch = slot_hit.astype(jnp.bfloat16)
    outgoing = jnp.einsum(
        "wct,td->wcd", dispatch, normed, preferred_element_type=jnp.float32
    ).astype(jnp.bfloat16)
    combine = jnp.where(slot_hit, token_weight[:, None, :], 0.0)
    shard_piece = lax.all_gather(outgoing, EP, axis=1, tiled=True)
    gate_act = jnp.einsum(
        "wnd,wfd->wnf", shard_piece, expert_gate, preferred_element_type=jnp.float32
    )
    up_act = jnp.einsum("wnd,wfd->wnf", shard_piece, expert_up, preferred_element_type=jnp.float32)
    activated = (jax.nn.silu(gate_act) * up_act).astype(jnp.bfloat16)
    partial_value = jnp.einsum(
        "wnf,wfd->wnd", activated, expert_down, preferred_element_type=jnp.float32
    )
    returned = summed_rows(partial_value.astype(jnp.bfloat16), ("ep_0", "ep_1"), "ep_2", 1).astype(
        jnp.float32
    )
    expert_mix = jnp.einsum("wct,wcd->td", combine, returned, precision=lax.Precision.HIGHEST)
    return (hidden_sum + expert_mix).astype(jnp.bfloat16)


def solution(mesh):
    finer = Mesh(mesh.devices.reshape(4, 2, 4, 2, 2), ("sp_0", "sp_1", "ep_0", "ep_1", "ep_2"))
    in_specs = (
        P(SP_EP, None),
        P(SP_EP, None),
        P(SP_EP, None),
        P(SP_EP, None),
        P(),
        P(SP_EP, None),
        P(),
        P(SP_EP, None),
        P(SP_EP, None),
        P(None, EP, None),
        P(None, EP, None),
        P(None, EP, None),
    )
    out_specs = P(SP_EP, None)
    return jax.shard_map(local, mesh=finer, in_specs=in_specs, out_specs=out_specs, check_vma=False)
```

profile of v0, /device:TPU:0, one launch (start us, length us, event | category | flops | bytes accessed | tf_op | source)
XLA Modules:
  0.0 554.0 jit_solution(9617605456632992405)
XLA Ops:
  6.5 1.1 copy.87
  7.7 0.9 copy.88
  8.5 5.4 all-to-all-start
  13.9 1.1 copy.89
  15.1 0.9 copy.90
  15.9 5.2 all-to-all-done
  21.2 3.4 all-to-all-start.1
  24.6 0.7 all-gather.3.cloned.1.call-update
  25.3 0.8 reshape.128
  26.1 2.3 copy.100
  28.4 3.1 all-to-all-done.1
  31.4 4.2 all-to-all-start.2
  35.7 0.9 pad_maximum_fusion
  36.6 2.9 collective-permute-start.1
  39.5 4.3 collective-permute-start.2
  43.8 0.1 constant_dynamic-slice_fusion
  43.9 0.1 copy.116
  44.1 0.1 broadcast_or_fusion
  44.2 2.0 collective-permute-start.3
  46.2 18.2 %collective-permute-done = bf16[8,128,256]{2,1,0:T(8,128)(2,1)S(1)} collective-permute-done((bf16[8,128,256]{2,1,0:T(8,128)(2,1)}, bf16[8,128,256]{2,1,0:T(8,128)(2,1)S(1)}, u32[]{:S(2)}, u32[]{:S(2)}) %collective-permute-start) | collective-permute-done | bytes 524320 | tf_op jit(solution)/shard_map/ppermute | solution.py:18
  64.4 2.3 collective-permute-done.1
  66.7 8.3 %collective-permute-start.6 = (bf16[8,128,256]{2,1,0:T(8,128)(2,1)}, bf16[8,128,256]{2,1,0:T(8,128)(2,1)}, u32[]{:S(2)}, u32[]{:S(2)}) collective-permute-start(bf16[8,128,256]{2,1,0:T(8,128)(2,1)} %pad_maximum_fusion), channel_id=1, source_target_pairs={{0,7},{1,8},{2,9},{3,10},{4,11},{5,12},{6,13},{7,14},{8,15},{9,0},... | collective-permute-start | bytes 1572872 | tf_op jit(solution)/shard_map/ppermute | solution.py:18
  75.0 25.7 %collective-permute-done.2 = bf16[8,128,256]{2,1,0:T(8,128)(2,1)S(1)} collective-permute-done((bf16[8,128,256]{2,1,0:T(8,128)(2,1)}, bf16[8,128,256]{2,1,0:T(8,128)(2,1)S(1)}, u32[]{:S(2)}, u32[]{:S(2)}) %collective-permute-start.2) | collective-permute-done | bytes 524320 | tf_op jit(solution)/shard_map/ppermute | solution.py:18
  100.7 0.6 broadcast_and_fusion
  101.4 0.8 bitcast_dynamic-update-slice_fusion.7
  102.3 5.5 collective-permute-done.3
  107.8 1.0 slice.43
  108.9 8.1 %collective-permute-done.4 = bf16[8,128,256]{2,1,0:T(8,128)(2,1)} collective-permute-done((bf16[8,128,256]{2,1,0:T(8,128)(2,1)}, bf16[8,128,256]{2,1,0:T(8,128)(2,1)}, u32[]{:S(2)}, u32[]{:S(2)}) %collective-permute-start.4) | collective-permute-done | bytes 524320 | tf_op jit(solution)/shard_map/ppermute | solution.py:18
  117.0 1.0 slice.44
  118.0 1.0 slice.45
  119.1 5.4 collective-permute-done.6
  124.5 1.0 slice.46
  125.5 9.7 %collective-permute-done.7 = bf16[8,128,256]{2,1,0:T(8,128)(2,1)} collective-permute-done((bf16[8,128,256]{2,1,0:T(8,128)(2,1)}, bf16[8,128,256]{2,1,0:T(8,128)(2,1)}, u32[]{:S(2)}, u32[]{:S(2)}) %collective-permute-start.7) | collective-permute-done | bytes 524320 | tf_op jit(solution)/shard_map/ppermute | solution.py:18
  135.2 1.1 slice.47
  136.2 0.9 bitcast_dynamic-update-slice_fusion.6
  137.1 0.9 bitcast_dynamic-update-slice_fusion.5
  138.1 0.9 bitcast_dynamic-update-slice_fusion.4
  139.0 0.9 bitcast_dynamic-update-slice_fusion.3
  139.9 0.9 bitcast_dynamic-update-slice_fusion.2
  140.8 0.9 bitcast_dynamic-update-slice_fusion.1
  141.8 0.9 bitcast_dynamic-update-slice_fusion
  142.7 0.9 bitcast_dynamic-update-slice_fusion.8
  143.6 4.8 fusion
  148.4 5.0 fusion.1
  153.4 1.5 copy-done
  154.9 9.7 %fusion.10 = bf16[8,128,1,4,128]{1,4,3,0,2:T(8,128)(2,1)S(1)} fusion(f32[8,9,128,128,4]{3,2,4,1,0:T(8,128)} %copy-done, f32[8,4,128]{2,1,0:T(4,128)S(1)} %get-tuple-element.5, pred[8,128,9,128]{1,3,2,0:T(8,128)(4,1)S(1)} %broadcast_and_fusion, bf16[9,8,128,256]{3,2,0,1:T(8,128)(2,1)} %bitcast_dynamic-update-slice_fusion.8, f32[8,128,4]{1,2,0:T(4,128)S(1)} %bitcast.157), kind=kOutput, calls=%fused_computation.20 | convolution fusion | flops 1232601088 | bytes 23494656 | tf_op jit(solution)/shard_map/sgrtdu,dsugh->stgrh/dot_general | solution.py:110
  164.6 0.7 copy.104
  165.3 9.0 %convolution_convert_fusion.1 = bf16[1024,4096]{1,0:T(8,128)(2,1)} fusion(bf16[512,4096]{1,0:T(8,128)(2,1)} %all-gather.3.cloned.1.call-done, bf16[64,8,8,128]{3,2,1,0:T(8,128)(2,1)S(1)} %bitcast.154), kind=kOutput, calls=%fused_computation.9 | convolution fusion | flops 4299161600 | bytes 13631488 | tf_op jit(solution)/shard_map/dot_general | solution.py:116
  174.4 0.0 reduce-scatter.7.cloned.1.call-start
  174.4 85.9 %reduce-scatter.5.cloned.1.call-done = bf16[256,4096]{1,0:T(8,128)(2,1)} async-done(((bf16[1024,4096]{1,0:T(8,128)(2,1)}), bf16[256,4096]{1,0:T(8,128)(2,1)}) %reduce-scatter.5.cloned.1.call-update) | async-done | bytes 2097168 | tf_op jit(solution)/shard_map/reduce_scatter | solution.py:24
  260.5 0.3 reduce_window_sum.11
  260.8 36.1 %reduce-scatter.7.cloned.1.call-done = bf16[128,4096]{1,0:T(8,128)(2,1)} async-done(((bf16[256,4096]{1,0:T(8,128)(2,1)}), bf16[128,4096]{1,0:T(8,128)(2,1)}) %reduce-scatter.7.cloned.1.call-update) | async-done | bytes 1048592 | tf_op jit(solution)/shard_map/reduce_scatter | solution.py:24
  296.9 1.6 multiply_reduce_fusion
  298.6 2.7 convolution_convert_fusion.2
  301.3 0.3 reduce-scatter.9.cloned.1.call-start
  301.6 82.6 %all-gather.5.cloned.1.call-done = bf16[2,640,4096]{2,1,0:T(8,128)(2,1)} async-done(((bf16[2,40,4096]{2,1,0:T(8,128)(2,1)}), bf16[2,640,4096]{2,1,0:T(8,128)(2,1)}) %all-gather.5.cloned.1.call-update) | async-done | bytes 10485776 | tf_op jit(solution)/shard_map/all_gather | solution.py:134
  384.1 13.0 %fusion.35 = f32[2,640,448]{1,2,0:T(8,128)} fusion(bf16[2,640,4096]{2,1,0:T(8,128)(2,1)} %all-gather.5.cloned.1.call-done, bf16[2,448,4096]{2,1,0:T(8,128)(2,1)} %param.21), kind=kOutput, calls=%fused_computation.63 | convolution fusion | flops 4697620480 | bytes 20119552 | tf_op jit(solution)/shard_map/wnd,wfd->wnf/dot_general | solution.py:135
  397.1 12.4 %multiply_convert_fusion = bf16[2,640,448]{1,2,0:T(8,128)(2,1)S(1)} fusion(f32[2,640,448]{1,2,0:T(8,128)} %fusion.35, bf16[2,640,4096]{2,1,0:T(8,128)(2,1)} %all-gather.5.cloned.1.call-done, bf16[2,448,4096]{2,1,0:T(8,128)(2,1)} %param.22), kind=kOutput, calls=%fused_computation.18 | convolution fusion | flops 4701061120 | bytes 21266432 | tf_op jit(solution)/shard_map/wnd,wfd->wnf/dot_general | solution.py:138
  409.5 10.2 %convolution_convert_fusion = bf16[2,640,4096]{2,1,0:T(8,128)(2,1)} fusion(bf16[2,640,448]{1,2,0:T(8,128)(2,1)S(1)} %multiply_convert_fusion, bf16[2,448,4096]{2,1,0:T(8,128)(2,1)} %param.23), kind=kOutput, calls=%fused_computation.8 | convolution fusion | flops 4702863360 | bytes 18972672 | tf_op jit(solution)/shard_map/wnf,wfd->wnd/dot_general | solution.py:140
  419.7 9.6 %copy.105 = bf16[8,2,2,40,4096]{4,3,2,0,1:T(8,128)(2,1)} copy(bf16[8,2,2,40,4096]{4,3,1,0,2:T(8,128)(2,1)} %bitcast.149) | data formatting | bytes 20971520 | tf_op jit(solution)/shard_map/reshape | solution.py:37
  429.4 0.0 reduce-scatter.11.cloned.1.call-start
  429.4 18.5 %reduce-scatter.9.cloned.1.call-done = bf16[8,2,40,4096]{3,2,1,0:T(8,128)(2,1)} async-done(((bf16[16,2,40,4096]{3,2,1,0:T(8,128)(2,1)}), bf16[8,2,40,4096]{3,2,1,0:T(8,128)(2,1)}) %reduce-scatter.9.cloned.1.call-update) | async-done | bytes 5242896 | tf_op jit(solution)/shard_map/reduce_scatter | solution.py:38
  448.0 95.9 %reduce-scatter.11.cloned.1.call-done = bf16[1,2,40,4096]{3,2,1,0:T(8,128)(2,1)} async-done(((bf16[8,2,40,4096]{3,2,1,0:T(8,128)(2,1)}), bf16[1,2,40,4096]{3,2,1,0:T(8,128)(2,1)}) %reduce-scatter.11.cloned.1.call-update) | async-done | bytes 655376 | tf_op jit(solution)/shard_map/reduce_scatter | solution.py:39
  543.9 3.2 fusion.8
  (37 shorter events, 0.4 us)
Async XLA Ops:
  8.5 12.6 %all-to-all-start = ((bf16[1,128,8,128]{3,1,0,2:T(8,128)(2,1)}), bf16[1,128,8,128]{3,1,0,2:T(8,128)(2,1)S(1)}, u32[]{:S(2)}, u32[]{:S(2)}) async-start(bf16[1,128,8,128]{3,1,0,2:T(8,128)(2,1)} %copy.88), calls=%async_computation | async-start | bytes 524288 | tf_op jit(solution)/shard_map/all_to_all | solution.py:75
  21.2 10.3 %all-to-all-start.1 = ((bf16[1,128,8,128]{3,1,0,2:T(8,128)(2,1)}), bf16[1,128,8,128]{3,1,0,2:T(8,128)(2,1)S(1)}, u32[]{:S(2)}, u32[]{:S(2)}) async-start(bf16[1,128,8,128]{3,1,0,2:T(8,128)(2,1)} %copy.90), calls=%async_computation.1 | async-start | bytes 524288 | tf_op jit(solution)/shard_map/all_to_all | solution.py:76
  24.6 140.7 %all-gather.3.cloned.1.call-start = ((), (), s32[]{:S(2)}) async-start(), calls=%async_computation.7 | async-start | bytes 4456448 | tf_op jit(solution)/shard_map/all_gather | solution.py:115
  31.4 112.2 %all-to-all-start.2 = ((bf16[1,128,8,512]{1,3,0,2:T(8,128)(2,1)}), bf16[1,128,8,512]{1,3,0,2:T(8,128)(2,1)}, u32[]{:S(2)}, u32[]{:S(2)}) async-start(bf16[1,128,8,512]{1,3,0,2:T(8,128)(2,1)} %bitcast.29), calls=%async_computation.2 | async-start | bytes 2097152 | tf_op jit(solution)/shard_map/all_to_all | solution.py:74
  35.7 224.7 %reduce-scatter.5.cloned.1.call-start = ((), (), s32[]{:S(2)}) async-start(), calls=%async_computation.8 | async-start | bytes 10485760 | tf_op jit(solution)/shard_map/reduce_scatter | solution.py:24
  36.6 27.8 %collective-permute-start = (bf16[8,128,256]{2,1,0:T(8,128)(2,1)}, bf16[8,128,256]{2,1,0:T(8,128)(2,1)S(1)}, u32[]{:S(2)}, u32[]{:S(2)}) collective-permute-start(bf16[8,128,256]{2,1,0:T(8,128)(2,1)} %pad_maximum_fusion), channel_id=1, source_target_pairs={{0,1},{1,2},{2,3},{3,4},{4,5},{5,6},{6,7},{7,8},{8,9},{9,10},{10,1... | collective-permute-start | bytes 1572872 | tf_op jit(solution)/shard_map/ppermute | solution.py:18
  36.6 30.1 %collective-permute-start.1 = (bf16[8,128,256]{2,1,0:T(8,128)(2,1)}, bf16[8,128,256]{2,1,0:T(8,128)(2,1)S(1)}, u32[]{:S(2)}, u32[]{:S(2)}) collective-permute-start(bf16[8,128,256]{2,1,0:T(8,128)(2,1)} %pad_maximum_fusion), channel_id=1, source_target_pairs={{0,2},{1,3},{2,4},{3,5},{4,6},{5,7},{6,8},{7,9},{8,10},{9,11},{10,... | collective-permute-start | bytes 1572872 | tf_op jit(solution)/shard_map/ppermute | solution.py:18
  39.5 61.2 %collective-permute-start.2 = (bf16[8,128,256]{2,1,0:T(8,128)(2,1)}, bf16[8,128,256]{2,1,0:T(8,128)(2,1)S(1)}, u32[]{:S(2)}, u32[]{:S(2)}) collective-permute-start(bf16[8,128,256]{2,1,0:T(8,128)(2,1)} %pad_maximum_fusion), channel_id=1, source_target_pairs={{0,3},{1,4},{2,5},{3,6},{4,7},{5,8},{6,9},{7,10},{8,11},{9,12},{10... | collective-permute-start | bytes 1572872 | tf_op jit(solution)/shard_map/ppermute | solution.py:18
  44.2 63.6 %collective-permute-start.3 = (bf16[8,128,256]{2,1,0:T(8,128)(2,1)}, bf16[8,128,256]{2,1,0:T(8,128)(2,1)}, u32[]{:S(2)}, u32[]{:S(2)}) collective-permute-start(bf16[8,128,256]{2,1,0:T(8,128)(2,1)} %pad_maximum_fusion), channel_id=1, source_target_pairs={{0,4},{1,5},{2,6},{3,7},{4,8},{5,9},{6,10},{7,11},{8,12},{9,13},{1... | collective-permute-start | bytes 1572872 | tf_op jit(solution)/shard_map/ppermute | solution.py:18
  46.2 70.8 %collective-permute-start.4 = (bf16[8,128,256]{2,1,0:T(8,128)(2,1)}, bf16[8,128,256]{2,1,0:T(8,128)(2,1)}, u32[]{:S(2)}, u32[]{:S(2)}) collective-permute-start(bf16[8,128,256]{2,1,0:T(8,128)(2,1)} %pad_maximum_fusion), channel_id=1, source_target_pairs={{0,5},{1,6},{2,7},{3,8},{4,9},{5,10},{6,11},{7,12},{8,13},{9,14},{... | collective-permute-start | bytes 1572872 | tf_op jit(solution)/shard_map/ppermute | solution.py:18
  64.4 53.6 %collective-permute-start.5 = (bf16[8,128,256]{2,1,0:T(8,128)(2,1)}, bf16[8,128,256]{2,1,0:T(8,128)(2,1)}, u32[]{:S(2)}, u32[]{:S(2)}) collective-permute-start(bf16[8,128,256]{2,1,0:T(8,128)(2,1)} %pad_maximum_fusion), channel_id=1, source_target_pairs={{0,6},{1,7},{2,8},{3,9},{4,10},{5,11},{6,12},{7,13},{8,14},{9,15},... | collective-permute-start | bytes 1572872 | tf_op jit(solution)/shard_map/ppermute | solution.py:18
  66.7 57.7 %collective-permute-start.6 = (bf16[8,128,256]{2,1,0:T(8,128)(2,1)}, bf16[8,128,256]{2,1,0:T(8,128)(2,1)}, u32[]{:S(2)}, u32[]{:S(2)}) collective-permute-start(bf16[8,128,256]{2,1,0:T(8,128)(2,1)} %pad_maximum_fusion), channel_id=1, source_target_pairs={{0,7},{1,8},{2,9},{3,10},{4,11},{5,12},{6,13},{7,14},{8,15},{9,0},... | collective-permute-start | bytes 1572872 | tf_op jit(solution)/shard_map/ppermute | solution.py:18
  100.7 34.5 %collective-permute-start.7 = (bf16[8,128,256]{2,1,0:T(8,128)(2,1)}, bf16[8,128,256]{2,1,0:T(8,128)(2,1)}, u32[]{:S(2)}, u32[]{:S(2)}) collective-permute-start(bf16[8,128,256]{2,1,0:T(8,128)(2,1)} %pad_maximum_fusion), channel_id=1, source_target_pairs={{0,8},{1,9},{2,10},{3,11},{4,12},{5,13},{6,14},{7,15},{8,0},{9,1},... | collective-permute-start | bytes 1572872 | tf_op jit(solution)/shard_map/ppermute | solution.py:18
  148.4 6.5 %copy-start = (f32[8,9,128,128,4]{3,2,4,1,0:T(8,128)}, f32[8,9,128,128,4]{3,2,4,1,0:T(8,128)S(1)}, u32[]{:S(2)}) copy-start(f32[8,9,128,128,4]{3,2,4,1,0:T(8,128)S(1)} %get-tuple-element.6) | copy-start | bytes 56623108
  174.3 86.1 %copy-start.4 = (s32[128,2]{0,1:T(2,128)S(1)}, s32[128,2]{0,1:T(2,128)}, u32[]{:S(2)}) copy-start(s32[128,2]{0,1:T(2,128)} %param.19) | copy-start | bytes 3076
  174.3 122.6 %copy-start.1 = (bf16[128,4096]{1,0:T(8,128)(2,1)S(1)}, bf16[128,4096]{1,0:T(8,128)(2,1)}, u32[]{:S(2)}) copy-start(bf16[128,4096]{1,0:T(8,128)(2,1)} %param.12) | copy-start | bytes 3145732
  174.3 124.2 %copy-start.3 = (f32[4096]{0:T(1024)S(1)}, f32[4096]{0:T(1024)}, u32[]{:S(2)}) copy-start(f32[4096]{0:T(1024)} %param.18) | copy-start | bytes 49156
  174.4 122.6 %reduce-scatter.7.cloned.1.call-start = ((), (), s32[]{:S(2)}) async-start(), calls=%async_computation.9 | async-start | bytes 3145728 | tf_op jit(solution)/shard_map/reduce_scatter | solution.py:24
  260.4 123.7 %all-gather.5.cloned.1.call-start = ((), (), s32[]{:S(2)}) async-start(), calls=%async_computation.10 | async-start | bytes 11141120 | tf_op jit(solution)/shard_map/all_gather | solution.py:134
  301.3 146.6 %reduce-scatter.9.cloned.1.call-start = ((), (), s32[]{:S(2)}) async-start(), calls=%async_computation.11 | async-start | bytes 15728640 | tf_op jit(solution)/shard_map/reduce_scatter | solution.py:38
  429.3 18.6 %copy-start.5 = (f32[128,2]{0,1:T(2,128)S(1)}, f32[128,2]{0,1:T(2,128)}, u32[]{:S(2)}) copy-start(f32[128,2]{0,1:T(2,128)} %param.20) | copy-start | bytes 3076
  429.4 114.6 %copy-start.2 = (bf16[128,4096]{1,0:T(8,128)(2,1)S(1)}, bf16[128,4096]{1,0:T(8,128)(2,1)}, u32[]{:S(2)}) copy-start(bf16[128,4096]{1,0:T(8,128)(2,1)} %reduce-scatter.7.cloned.1.call-done) | copy-start | bytes 3145732
  429.4 114.6 %reduce-scatter.11.cloned.1.call-start = ((), (), s32[]{:S(2)}) async-start(), calls=%async_computation.12 | async-start | bytes 5898240 | tf_op jit(solution)/shard_map/reduce_scatter | solution.py:39
Sparse Core Ops, SparseCore 0:
  27.8 117.8 all-gather.2
  174.5 85.8 reduce-scatter.4
  262.7 34.1 reduce-scatter.6
  301.4 82.6 all-gather.4
  429.5 18.4 reduce-scatter.8
  451.6 92.2 reduce-scatter.10
where the time goes:
time: 555 us; the launch traced here: 554 us
  waiting for transfers between devices  403 us (73%)
  matrix products  64.9 us (12%)
  starting transfers between devices  31 us (6%)
  local copies, waits for them, and re-layouts  24.3 us (4%)
  other arithmetic  16.9 us (3%)
  between operations  13.7 us (2%)
    reduce_scatter x2, waiting for transfers between devices, sum_by_axis(): total = lax.psum_scatter(total, axis, scatter_dimension=0, tiled=True)  122 us
    reduce_scatter x1, waiting for transfers between devices, summed_rows(): return lax.psum_scatter(blocks, chips, scatter_dimension=0, tiled=True)[0]  95.9 us
    all_gather x1, waiting for transfers between devices, local(): shard_piece = lax.all_gather(outgoing, EP, axis=1, tiled=True)  82.6 us
    ppermute x8, waiting for transfers between devices, shifted(): return lax.ppermute(value, axis, pairs)  74.9 us
    reduce_scatter x1, waiting for transfers between devices, summed_rows(): blocks = lax.psum_scatter(blocks, core, scatter_dimension=0, tiled=True)  18.5 us
    ppermute x8, starting transfers between devices, shifted(): return lax.ppermute(value, axis, pairs)  17.5 us
    dot_general x1, matrix products, local(): jnp.einsum('wnd,wfd->wnf', shard_piece, expert_gate, preferred_element_ty...  13 us
    dot_general x1, matrix products, local(): jnp.einsum('wnd,wfd->wnf', shard_piece, expert_up, preferred_element_type...  12.4 us
  transfers between devices with their start and end apart: 17, of which 14 were waited for; matrix products, arithmetic and copies ran while one was open for 7% of the time, Pallas kernels for 0%

commit v1 on v0

--- a/solution.py
+++ b/solution.py
@@ -131,7 +131,9 @@
         "wct,td->wcd", dispatch, normed, preferred_element_type=jnp.float32
     ).astype(jnp.bfloat16)
     combine = jnp.where(slot_hit, token_weight[:, None, :], 0.0)
-    shard_piece = lax.all_gather(outgoing, EP, axis=1, tiled=True)
+    shard_piece = jnp.concatenate(
+        lax.all_to_all(jnp.stack([outgoing] * lax.axis_size(EP)), EP, 0, 0), axis=1
+    )
     gate_act = jnp.einsum(
         "wnd,wfd->wnf", shard_piece, expert_gate, preferred_element_type=jnp.float32
     )

time: 555 us -> 608 us (1.095)
  blocking collectives: 0 us -> 126 us
  waiting for transfers between devices: 403 us -> 320 us
  local copies, waits for them, and re-layouts: 24.3 us -> 35.1 us
    all_to_all x0 -> x1, blocking collectives: none -> 126 us  [local(): lax.all_to_all(jnp.stack([outgoing] * lax.axis_size(EP)), EP, 0, 0)]
    all_gather x1 -> x0, waiting for transfers between devices: 82.6 us -> none  [local(): shard_piece = lax.all_gather(outgoing, EP, axis=1, tiled=True)]
    reshape x0 -> x1, local copies, waits for them, and re-layouts: none -> 9.59 us  [local(): jnp.concatenate(lax.all_to_all(jnp.stack([outgoing] * lax.axis_size(EP)),...]
  transfers between devices with their start and end apart: 17 -> 16, of which waited for: 14 -> 13; matrix products, arithmetic and copies ran while one was open for 7% -> 7% of each run, Pallas kernels for 0% -> 0%
where the time goes in v1:
time: 608 us; the launch traced here: 607 us
  waiting for transfers between devices  320 us (53%)
  blocking collectives  126 us (21%)
  matrix products  65.6 us (11%)
  local copies, waits for them, and re-layouts  35.1 us (6%)
  starting transfers between devices  30.8 us (5%)
  other arithmetic  16.9 us (3%)
  between operations  13.4 us (2%)
    all_to_all x1, blocking collectives, local(): lax.all_to_all(jnp.stack([outgoing] * lax.axis_size(EP)), EP, 0, 0)  126 us
    reduce_scatter x2, waiting for transfers between devices, sum_by_axis(): total = lax.psum_scatter(total, axis, scatter_dimension=0, tiled=True)  122 us
    reduce_scatter x1, waiting for transfers between devices, summed_rows(): return lax.psum_scatter(blocks, chips, scatter_dimension=0, tiled=True)[0]  95.9 us
    ppermute x8, waiting for transfers between devices, shifted(): return lax.ppermute(value, axis, pairs)  74.9 us
    reduce_scatter x1, waiting for transfers between devices, summed_rows(): blocks = lax.psum_scatter(blocks, core, scatter_dimension=0, tiled=True)  17.7 us
    ppermute x8, starting transfers between devices, shifted(): return lax.ppermute(value, axis, pairs)  17.5 us
    dot_general x1, matrix products, local(): jnp.einsum('wnd,wfd->wnf', shard_piece, expert_gate, preferred_element_ty...  13.5 us
    dot_general x1, matrix products, local(): jnp.einsum('wnd,wfd->wnf', shard_piece, expert_up, preferred_element_type...  12.9 us
  transfers between devices with their start and end apart: 16, of which 13 were waited for; matrix products, arithmetic and copies ran while one was open for 7% of the time, Pallas kernels for 0%

profile of v1, /device:TPU:0, one launch (start us, length us, event | category | flops | bytes accessed | tf_op | source)
XLA Modules:
  0.0 607.1 jit_solution(11504001402883737889)
XLA Ops:
  6.5 1.1 copy.89
  7.7 0.9 copy.90
  8.5 5.4 all-to-all-start
  13.9 1.1 copy.91
  15.1 0.9 copy.92
  15.9 5.2 all-to-all-done
  21.2 3.4 all-to-all-start.1
  24.6 0.7 all-gather.2.cloned.1.call-update
  25.3 0.8 reshape.136
  26.1 2.3 copy.102
  28.4 3.1 all-to-all-done.1
  31.4 4.2 all-to-all-start.2
  35.7 0.8 pad_maximum_fusion
  36.6 2.9 collective-permute-start.1
  39.5 4.3 collective-permute-start.2
  43.8 0.1 constant_dynamic-slice_fusion
  43.9 0.1 copy.119
  44.1 0.1 broadcast_or_fusion
  44.2 2.0 collective-permute-start.3
  46.2 18.2 %collective-permute-done = bf16[8,128,256]{2,1,0:T(8,128)(2,1)S(1)} collective-permute-done((bf16[8,128,256]{2,1,0:T(8,128)(2,1)}, bf16[8,128,256]{2,1,0:T(8,128)(2,1)S(1)}, u32[]{:S(2)}, u32[]{:S(2)}) %collective-permute-start) | collective-permute-done | bytes 524320 | tf_op jit(solution)/shard_map/ppermute | solution.py:18
  64.4 2.3 collective-permute-done.1
  66.7 8.3 %collective-permute-start.6 = (bf16[8,128,256]{2,1,0:T(8,128)(2,1)}, bf16[8,128,256]{2,1,0:T(8,128)(2,1)}, u32[]{:S(2)}, u32[]{:S(2)}) collective-permute-start(bf16[8,128,256]{2,1,0:T(8,128)(2,1)} %pad_maximum_fusion), channel_id=1, source_target_pairs={{0,7},{1,8},{2,9},{3,10},{4,11},{5,12},{6,13},{7,14},{8,15},{9,0},... | collective-permute-start | bytes 1572872 | tf_op jit(solution)/shard_map/ppermute | solution.py:18
  75.0 25.7 %collective-permute-done.2 = bf16[8,128,256]{2,1,0:T(8,128)(2,1)S(1)} collective-permute-done((bf16[8,128,256]{2,1,0:T(8,128)(2,1)}, bf16[8,128,256]{2,1,0:T(8,128)(2,1)S(1)}, u32[]{:S(2)}, u32[]{:S(2)}) %collective-permute-start.2) | collective-permute-done | bytes 524320 | tf_op jit(solution)/shard_map/ppermute | solution.py:18
  100.7 0.6 broadcast_and_fusion
  101.3 0.9 bitcast_dynamic-update-slice_fusion.7
  102.3 5.5 collective-permute-done.3
  107.8 1.0 slice.43
  108.9 8.1 %collective-permute-done.4 = bf16[8,128,256]{2,1,0:T(8,128)(2,1)} collective-permute-done((bf16[8,128,256]{2,1,0:T(8,128)(2,1)}, bf16[8,128,256]{2,1,0:T(8,128)(2,1)}, u32[]{:S(2)}, u32[]{:S(2)}) %collective-permute-start.4) | collective-permute-done | bytes 524320 | tf_op jit(solution)/shard_map/ppermute | solution.py:18
  117.0 1.0 slice.44
  118.0 1.0 slice.45
  119.1 5.4 collective-permute-done.6
  124.5 1.0 slice.46
  125.5 9.7 %collective-permute-done.7 = bf16[8,128,256]{2,1,0:T(8,128)(2,1)} collective-permute-done((bf16[8,128,256]{2,1,0:T(8,128)(2,1)}, bf16[8,128,256]{2,1,0:T(8,128)(2,1)}, u32[]{:S(2)}, u32[]{:S(2)}) %collective-permute-start.7) | collective-permute-done | bytes 524320 | tf_op jit(solution)/shard_map/ppermute | solution.py:18
  135.2 1.1 slice.47
  136.2 0.9 bitcast_dynamic-update-slice_fusion.6
  137.1 0.9 bitcast_dynamic-update-slice_fusion.5
  138.0 0.9 bitcast_dynamic-update-slice_fusion.4
  139.0 0.9 bitcast_dynamic-update-slice_fusion.3
  139.9 0.9 bitcast_dynamic-update-slice_fusion.2
  140.8 0.9 bitcast_dynamic-update-slice_fusion.1
  141.8 0.9 bitcast_dynamic-update-slice_fusion
  142.7 0.9 bitcast_dynamic-update-slice_fusion.8
  143.6 4.8 fusion
  148.4 5.0 fusion.1
  153.4 1.5 copy-done
  154.9 9.7 %fusion.10 = bf16[8,128,1,4,128]{1,4,3,0,2:T(8,128)(2,1)S(1)} fusion(f32[8,9,128,128,4]{3,2,4,1,0:T(8,128)} %copy-done, f32[8,4,128]{2,1,0:T(4,128)S(1)} %get-tuple-element.5, pred[8,128,9,128]{1,3,2,0:T(8,128)(4,1)S(1)} %broadcast_and_fusion, bf16[9,8,128,256]{3,2,0,1:T(8,128)(2,1)} %bitcast_dynamic-update-slice_fusion.8, f32[8,128,4]{1,2,0:T(4,128)S(1)} %bitcast.162), kind=kOutput, calls=%fused_computation.20 | convolution fusion | flops 1232601088 | bytes 23494656 | tf_op jit(solution)/shard_map/sgrtdu,dsugh->stgrh/dot_general | solution.py:110
  164.6 0.7 copy.106
  165.3 9.0 %convolution_convert_fusion.1 = bf16[1024,4096]{1,0:T(8,128)(2,1)} fusion(bf16[512,4096]{1,0:T(8,128)(2,1)} %all-gather.2.cloned.1.call-done, bf16[64,8,8,128]{3,2,1,0:T(8,128)(2,1)S(1)} %bitcast.159), kind=kOutput, calls=%fused_computation.9 | convolution fusion | flops 4299161600 | bytes 13631488 | tf_op jit(solution)/shard_map/dot_general | solution.py:116
  174.4 85.9 %reduce-scatter.5.cloned.1.call-done = bf16[256,4096]{1,0:T(8,128)(2,1)} async-done(((bf16[1024,4096]{1,0:T(8,128)(2,1)}), bf16[256,4096]{1,0:T(8,128)(2,1)}) %reduce-scatter.5.cloned.1.call-update) | async-done | bytes 2097168 | tf_op jit(solution)/shard_map/reduce_scatter | solution.py:24
  260.5 0.3 reduce_window_sum.11
  260.8 36.1 %reduce-scatter.7.cloned.1.call-done = bf16[128,4096]{1,0:T(8,128)(2,1)} async-done(((bf16[256,4096]{1,0:T(8,128)(2,1)}), bf16[128,4096]{1,0:T(8,128)(2,1)}) %reduce-scatter.7.cloned.1.call-update) | async-done | bytes 1048592 | tf_op jit(solution)/shard_map/reduce_scatter | solution.py:24
  296.9 1.6 multiply_reduce_fusion
  298.6 1.8 convolution_convert_fusion.2
  300.4 1.3 stack.59
  301.7 125.7 %all_to_all.50 = bf16[16,2,40,4096]{3,2,1,0:T(8,128)(2,1)} all-to-all(bf16[16,2,40,4096]{3,2,1,0:T(8,128)(2,1)S(1)} %stack.59), channel_id=1, replica_groups=mesh['sp_0'=4,'sp_1'=2,'ep_0'=4,'ep_1'=2,'ep_2'=2] {'ep_0','ep_1','ep_2'}, dimensions={0} | all-to-all | bytes 20971520 | tf_op jit(solution)/shard_map/all_to_all | solution.py:135
  427.4 9.6 %copy.107 = bf16[2,16,40,4096]{3,2,1,0:T(8,128)(2,1)} copy(bf16[2,16,40,4096]{3,2,0,1:T(8,128)(2,1)} %bitcast.151) | data formatting | bytes 20971520 | tf_op jit(solution)/shard_map/reshape | solution.py:134
  437.0 13.5 %fusion.35 = f32[2,640,448]{1,2,0:T(8,128)S(1)} fusion(bf16[2,640,4096]{2,1,0:T(8,128)(2,1)} %bitcast.152, bf16[2,448,4096]{2,1,0:T(8,128)(2,1)} %param.21), kind=kOutput, calls=%fused_computation.63 | convolution fusion | flops 4697620480 | bytes 20119552 | tf_op jit(solution)/shard_map/wnd,wfd->wnf/dot_general | solution.py:137
  450.5 12.9 %multiply_convert_fusion = bf16[2,640,448]{1,2,0:T(8,128)(2,1)} fusion(f32[2,640,448]{1,2,0:T(8,128)S(1)} %fusion.35, bf16[2,640,4096]{2,1,0:T(8,128)(2,1)} %bitcast.153, bf16[2,448,4096]{2,1,0:T(8,128)(2,1)} %param.22), kind=kOutput, calls=%fused_computation.18 | convolution fusion | flops 4701061120 | bytes 21266432 | tf_op jit(solution)/shard_map/wnd,wfd->wnf/dot_general | solution.py:140
  463.5 10.6 %convolution_convert_fusion = bf16[2,640,4096]{2,1,0:T(8,128)(2,1)} fusion(bf16[2,640,448]{1,2,0:T(8,128)(2,1)} %multiply_convert_fusion, bf16[2,448,4096]{2,1,0:T(8,128)(2,1)} %param.23), kind=kOutput, calls=%fused_computation.8 | convolution fusion | flops 4702863360 | bytes 18972672 | tf_op jit(solution)/shard_map/wnf,wfd->wnd/dot_general | solution.py:142
  474.1 9.5 %copy.108 = bf16[8,2,2,40,4096]{4,3,2,0,1:T(8,128)(2,1)} copy(bf16[8,2,2,40,4096]{4,3,1,0,2:T(8,128)(2,1)} %bitcast.154) | data formatting | bytes 20971520 | tf_op jit(solution)/shard_map/reshape | solution.py:37
  483.6 0.0 reduce-scatter.11.cloned.1.call-start
  483.6 17.7 %reduce-scatter.9.cloned.1.call-done = bf16[8,2,40,4096]{3,2,1,0:T(8,128)(2,1)} async-done(((bf16[16,2,40,4096]{3,2,1,0:T(8,128)(2,1)}), bf16[8,2,40,4096]{3,2,1,0:T(8,128)(2,1)}) %reduce-scatter.9.cloned.1.call-update) | async-done | bytes 5242896 | tf_op jit(solution)/shard_map/reduce_scatter | solution.py:38
  501.4 95.9 %reduce-scatter.11.cloned.1.call-done = bf16[1,2,40,4096]{3,2,1,0:T(8,128)(2,1)} async-done(((bf16[8,2,40,4096]{3,2,1,0:T(8,128)(2,1)}), bf16[1,2,40,4096]{3,2,1,0:T(8,128)(2,1)}) %reduce-scatter.11.cloned.1.call-update) | async-done | bytes 655376 | tf_op jit(solution)/shard_map/reduce_scatter | solution.py:39
  597.4 3.2 fusion.8
  (39 shorter events, 0.5 us)
Async XLA Ops:
  8.5 12.6 %all-to-all-start = ((bf16[1,128,8,128]{3,1,0,2:T(8,128)(2,1)}), bf16[1,128,8,128]{3,1,0,2:T(8,128)(2,1)S(1)}, u32[]{:S(2)}, u32[]{:S(2)}) async-start(bf16[1,128,8,128]{3,1,0,2:T(8,128)(2,1)} %copy.90), calls=%async_computation | async-start | bytes 524288 | tf_op jit(solution)/shard_map/all_to_all | solution.py:75
  21.2 10.3 %all-to-all-start.1 = ((bf16[1,128,8,128]{3,1,0,2:T(8,128)(2,1)}), bf16[1,128,8,128]{3,1,0,2:T(8,128)(2,1)S(1)}, u32[]{:S(2)}, u32[]{:S(2)}) async-start(bf16[1,128,8,128]{3,1,0,2:T(8,128)(2,1)} %copy.92), calls=%async_computation.1 | async-start | bytes 524288 | tf_op jit(solution)/shard_map/all_to_all | solution.py:76
  24.6 140.7 %all-gather.2.cloned.1.call-start = ((), (), s32[]{:S(2)}) async-start(), calls=%async_computation.8 | async-start | bytes 4456448 | tf_op jit(solution)/shard_map/all_gather | solution.py:115
  31.4 112.2 %all-to-all-start.2 = ((bf16[1,128,8,512]{1,3,0,2:T(8,128)(2,1)}), bf16[1,128,8,512]{1,3,0,2:T(8,128)(2,1)}, u32[]{:S(2)}, u32[]{:S(2)}) async-start(bf16[1,128,8,512]{1,3,0,2:T(8,128)(2,1)} %bitcast.29), calls=%async_computation.2 | async-start | bytes 2097152 | tf_op jit(solution)/shard_map/all_to_all | solution.py:74
  35.7 224.7 %reduce-scatter.5.cloned.1.call-start = ((), (), s32[]{:S(2)}) async-start(), calls=%async_computation.9 | async-start | bytes 10485760 | tf_op jit(solution)/shard_map/reduce_scatter | solution.py:24
  36.6 27.8 %collective-permute-start = (bf16[8,128,256]{2,1,0:T(8,128)(2,1)}, bf16[8,128,256]{2,1,0:T(8,128)(2,1)S(1)}, u32[]{:S(2)}, u32[]{:S(2)}) collective-permute-start(bf16[8,128,256]{2,1,0:T(8,128)(2,1)} %pad_maximum_fusion), channel_id=1, source_target_pairs={{0,1},{1,2},{2,3},{3,4},{4,5},{5,6},{6,7},{7,8},{8,9},{9,10},{10,1... | collective-permute-start | bytes 1572872 | tf_op jit(solution)/shard_map/ppermute | solution.py:18
  36.6 30.1 %collective-permute-start.1 = (bf16[8,128,256]{2,1,0:T(8,128)(2,1)}, bf16[8,128,256]{2,1,0:T(8,128)(2,1)S(1)}, u32[]{:S(2)}, u32[]{:S(2)}) collective-permute-start(bf16[8,128,256]{2,1,0:T(8,128)(2,1)} %pad_maximum_fusion), channel_id=1, source_target_pairs={{0,2},{1,3},{2,4},{3,5},{4,6},{5,7},{6,8},{7,9},{8,10},{9,11},{10,... | collective-permute-start | bytes 1572872 | tf_op jit(solution)/shard_map/ppermute | solution.py:18
  39.5 61.2 %collective-permute-start.2 = (bf16[8,128,256]{2,1,0:T(8,128)(2,1)}, bf16[8,128,256]{2,1,0:T(8,128)(2,1)S(1)}, u32[]{:S(2)}, u32[]{:S(2)}) collective-permute-start(bf16[8,128,256]{2,1,0:T(8,128)(2,1)} %pad_maximum_fusion), channel_id=1, source_target_pairs={{0,3},{1,4},{2,5},{3,6},{4,7},{5,8},{6,9},{7,10},{8,11},{9,12},{10... | collective-permute-start | bytes 1572872 | tf_op jit(solution)/shard_map/ppermute | solution.py:18
  44.2 63.6 %collective-permute-start.3 = (bf16[8,128,256]{2,1,0:T(8,128)(2,1)}, bf16[8,128,256]{2,1,0:T(8,128)(2,1)}, u32[]{:S(2)}, u32[]{:S(2)}) collective-permute-start(bf16[8,128,256]{2,1,0:T(8,128)(2,1)} %pad_maximum_fusion), channel_id=1, source_target_pairs={{0,4},{1,5},{2,6},{3,7},{4,8},{5,9},{6,10},{7,11},{8,12},{9,13},{1... | collective-permute-start | bytes 1572872 | tf_op jit(solution)/shard_map/ppermute | solution.py:18
  46.2 70.8 %collective-permute-start.4 = (bf16[8,128,256]{2,1,0:T(8,128)(2,1)}, bf16[8,128,256]{2,1,0:T(8,128)(2,1)}, u32[]{:S(2)}, u32[]{:S(2)}) collective-permute-start(bf16[8,128,256]{2,1,0:T(8,128)(2,1)} %pad_maximum_fusion), channel_id=1, source_target_pairs={{0,5},{1,6},{2,7},{3,8},{4,9},{5,10},{6,11},{7,12},{8,13},{9,14},{... | collective-permute-start | bytes 1572872 | tf_op jit(solution)/shard_map/ppermute | solution.py:18
  64.4 53.6 %collective-permute-start.5 = (bf16[8,128,256]{2,1,0:T(8,128)(2,1)}, bf16[8,128,256]{2,1,0:T(8,128)(2,1)}, u32[]{:S(2)}, u32[]{:S(2)}) collective-permute-start(bf16[8,128,256]{2,1,0:T(8,128)(2,1)} %pad_maximum_fusion), channel_id=1, source_target_pairs={{0,6},{1,7},{2,8},{3,9},{4,10},{5,11},{6,12},{7,13},{8,14},{9,15},... | collective-permute-start | bytes 1572872 | tf_op jit(solution)/shard_map/ppermute | solution.py:18
  66.7 57.7 %collective-permute-start.6 = (bf16[8,128,256]{2,1,0:T(8,128)(2,1)}, bf16[8,128,256]{2,1,0:T(8,128)(2,1)}, u32[]{:S(2)}, u32[]{:S(2)}) collective-permute-start(bf16[8,128,256]{2,1,0:T(8,128)(2,1)} %pad_maximum_fusion), channel_id=1, source_target_pairs={{0,7},{1,8},{2,9},{3,10},{4,11},{5,12},{6,13},{7,14},{8,15},{9,0},... | collective-permute-start | bytes 1572872 | tf_op jit(solution)/shard_map/ppermute | solution.py:18
  100.7 34.5 %collective-permute-start.7 = (bf16[8,128,256]{2,1,0:T(8,128)(2,1)}, bf16[8,128,256]{2,1,0:T(8,128)(2,1)}, u32[]{:S(2)}, u32[]{:S(2)}) collective-permute-start(bf16[8,128,256]{2,1,0:T(8,128)(2,1)} %pad_maximum_fusion), channel_id=1, source_target_pairs={{0,8},{1,9},{2,10},{3,11},{4,12},{5,13},{6,14},{7,15},{8,0},{9,1},... | collective-permute-start | bytes 1572872 | tf_op jit(solution)/shard_map/ppermute | solution.py:18
  148.4 6.5 %copy-start = (f32[8,9,128,128,4]{3,2,4,1,0:T(8,128)}, f32[8,9,128,128,4]{3,2,4,1,0:T(8,128)S(1)}, u32[]{:S(2)}) copy-start(f32[8,9,128,128,4]{3,2,4,1,0:T(8,128)S(1)} %get-tuple-element.6) | copy-start | bytes 56623108
  174.3 86.1 %copy-start.5 = (s32[128,2]{0,1:T(2,128)S(1)}, s32[128,2]{0,1:T(2,128)}, u32[]{:S(2)}) copy-start(s32[128,2]{0,1:T(2,128)} %param.19) | copy-start | bytes 3076
  174.3 122.6 %copy-start.1 = (bf16[128,4096]{1,0:T(8,128)(2,1)S(1)}, bf16[128,4096]{1,0:T(8,128)(2,1)}, u32[]{:S(2)}) copy-start(bf16[128,4096]{1,0:T(8,128)(2,1)} %param.12) | copy-start | bytes 3145732
  174.3 124.2 %copy-start.4 = (f32[4096]{0:T(1024)S(1)}, f32[4096]{0:T(1024)}, u32[]{:S(2)}) copy-start(f32[4096]{0:T(1024)} %param.18) | copy-start | bytes 49156
  174.4 122.6 %reduce-scatter.7.cloned.1.call-start = ((), (), s32[]{:S(2)}) async-start(), calls=%async_computation.10 | async-start | bytes 3145728 | tf_op jit(solution)/shard_map/reduce_scatter | solution.py:24
  260.4 241.0 %reduce-scatter.9.cloned.1.call-start = ((), (), s32[]{:S(2)}) async-start(), calls=%async_computation.11 | async-start | bytes 15728640 | tf_op jit(solution)/shard_map/reduce_scatter | solution.py:38
  483.6 17.9 %copy-start.6 = (f32[128,2]{0,1:T(2,128)S(1)}, f32[128,2]{0,1:T(2,128)}, u32[]{:S(2)}) copy-start(f32[128,2]{0,1:T(2,128)} %param.20) | copy-start | bytes 3076
  483.6 113.8 %copy-start.2 = (bf16[128,4096]{1,0:T(8,128)(2,1)S(1)}, bf16[128,4096]{1,0:T(8,128)(2,1)}, u32[]{:S(2)}) copy-start(bf16[128,4096]{1,0:T(8,128)(2,1)} %param.12) | copy-start | bytes 3145732
  483.6 113.8 %copy-start.3 = (bf16[128,4096]{1,0:T(8,128)(2,1)S(1)}, bf16[128,4096]{1,0:T(8,128)(2,1)}, u32[]{:S(2)}) copy-start(bf16[128,4096]{1,0:T(8,128)(2,1)} %reduce-scatter.7.cloned.1.call-done) | copy-start | bytes 3145732
  483.6 113.8 %reduce-scatter.11.cloned.1.call-start = ((), (), s32[]{:S(2)}) async-start(), calls=%async_computation.12 | async-start | bytes 5898240 | tf_op jit(solution)/shard_map/reduce_scatter | solution.py:39
Sparse Core Ops, SparseCore 0:
  27.8 117.8 all-gather.1
  174.5 85.8 reduce-scatter.4
  262.7 34.1 reduce-scatter.6
  483.7 17.6 reduce-scatter.8
  505.1 92.2 reduce-scatter.10
